TPU v7x, 64 devices: a 2x2x8 block of a 4x4x8 slice. The times are simulated.
64 devices in a mesh: dp: 4 (over x, y), ep: 16 (over z, core).
Axes of the slice: x: 2, y: 2, z: 8, core: 2. Of those that a mesh axis runs over, the one named last changes fastest.
The devices are a block of a 4x4x8 slice.
Arguments:
- h0: bfloat16 [64, 128, 2048], P(('dp', 'ep')), parts along dimension 0
- idx: int32 [64, 128, 8], P(('dp', 'ep')), parts along dimension 0
- slot: int32 [64, 128, 8], P(('dp', 'ep')), parts along dimension 0
- norm_attn: bfloat16 [2048], replicated
- wq: bfloat16 [2048, 4096], replicated
- wk: bfloat16 [2048, 512], replicated
- wv: bfloat16 [2048, 512], replicated
- wo: bfloat16 [4096, 2048], replicated
- norm_ffn: bfloat16 [2048], replicated
- w1: bfloat16 [2048, 6144], replicated
- w3: bfloat16 [2048, 6144], replicated
- w2: bfloat16 [6144, 2048], replicated
- norm_moe: bfloat16 [2048], replicated
- wr: bfloat16 [2048, 128], replicated
- ue1: bfloat16 [128, 2048, 768], P('ep')
- ue3: bfloat16 [128, 2048, 768], P('ep')
- ue2: bfloat16 [128, 768, 2048], P('ep')
Outputs:
- output: bfloat16 [64, 128, 2048], P(('dp', 'ep')), parts along dimension 0
There are 4 independent parts. A program takes and returns all parts, laid end to end along the dimension named above; an argument that names none is the same for every part.
All inputs are finite; a program needn't handle non-finite values.
Results may differ from a plain program's by a relative error of at most 0.0127771.
Values are sent between devices in bfloat16 or wider.
A program may use at most 768 MiB of HBM per device.

v0:
```python
import jax
import jax.numpy as jnp
from jax import lax
from jax.sharding import PartitionSpec as P

HEAD = 128
EPS = 1e-6
ROPE_BASE = 10000.0


def _rms(x, w):
    xf = x.astype(jnp.float32)
    r = lax.rsqrt(jnp.mean(xf * xf, axis=-1, keepdims=True) + EPS)
    return (xf * r * w.astype(jnp.float32)).astype(jnp.bfloat16)


def _rope(x, cos, sin):
    h = HEAD // 2
    x1, x2 = x[..., :h], x[..., h:]
    return jnp.concatenate([x1 * cos - x2 * sin, x2 * cos + x1 * sin], axis=-1)


def _dense(h0, na, wq, wk, wv, wo, nf, w1, w3, w2):
    f32, bf = jnp.float32, jnp.bfloat16
    b, s, d = h0.shape
    nh = wq.shape[1] // HEAD
    nkvv = wk.shape[1] // HEAD
    pos = jnp.arange(s).astype(f32)
    inv = ROPE_BASE ** (-2.0 * jnp.arange(HEAD // 2).astype(f32) / HEAD)
    ang = pos[:, None] * inv[None, :]
    cos, sin = jnp.cos(ang)[:, None, :], jnp.sin(ang)[:, None, :]
    x = _rms(h0, na).reshape(b * s, d)
    q = _rope(jnp.dot(x, wq, preferred_element_type=f32).reshape(b, s, nh, HEAD), cos, sin).astype(bf)
    k = _rope(jnp.dot(x, wk, preferred_element_type=f32).reshape(b, s, nkvv, HEAD), cos, sin).astype(bf)
    v = jnp.dot(x, wv, preferred_element_type=f32).astype(bf).reshape(b, s, nkvv, HEAD)
    q = q.reshape(b, s, nkvv, nh // nkvv, HEAD)
    sc = jnp.einsum('bqgrd,bkgd->bgrqk', q, k, preferred_element_type=f32) * HEAD ** -0.5
    causal = jnp.arange(s)[:, None] >= jnp.arange(s)[None, :]
    sc = jnp.where(causal, sc, -jnp.inf)
    p = jax.nn.softmax(sc, axis=-1).astype(bf)
    o = jnp.einsum('bgrqk,bkgd->bqgrd', p, v, preferred_element_type=f32).astype(bf).reshape(b * s, nh * HEAD)
    a = (h0.reshape(b * s, d).astype(f32) + jnp.dot(o, wo, preferred_element_type=f32)).astype(bf)
    z = _rms(a, nf)
    hid = (jax.nn.silu(jnp.dot(z, w1, preferred_element_type=f32)) * jnp.dot(z, w3, preferred_element_type=f32)).astype(bf)
    return a.astype(f32) + jnp.dot(hid, w2, preferred_element_type=f32)


def _route(h0, nm, wr, idx):
    d = h0.shape[-1]
    k = idx.shape[-1]
    u = _rms(h0, nm).reshape(-1, d)
    logits = jnp.dot(u, wr, preferred_element_type=jnp.float32)
    g = jax.nn.softmax(jnp.take_along_axis(logits, idx.reshape(-1, k), axis=1), axis=-1)
    return u, g


def _experts(x, ue1, ue3, ue2):
    f32 = jnp.float32
    h1 = jnp.einsum('ecd,edf->ecf', x, ue1, preferred_element_type=f32)
    h3 = jnp.einsum('ecd,edf->ecf', x, ue3, preferred_element_type=f32)
    hid = (jax.nn.silu(h1) * h3).astype(jnp.bfloat16)
    return jnp.einsum('ecf,efd->ecd', hid, ue2, preferred_element_type=f32).astype(jnp.bfloat16)


def solution(mesh):
    G = mesh.shape['ep']

    def local(h0, idx, slot, na, wq, wk, wv, wo, nf, w1, w3, w2, nm, wr, ue1, ue3, ue2):
        f32 = jnp.float32
        b, s, d = h0.shape
        t = b * s
        k = idx.shape[-1]
        el = ue1.shape[0]
        e = el * G
        cap = 2 * t * k // e
        u, g = _route(h0, nm, wr, idx)
        ix = idx.reshape(t, k)
        sl = slot.reshape(t, k)
        rows = jnp.broadcast_to(jnp.arange(t, dtype=jnp.int32)[:, None], (t, k))
        tok = jnp.full((e, cap), t, jnp.int32).at[ix, sl].set(rows)
        send = jnp.take(u, tok, axis=0, mode='fill', fill_value=0)
        recv = lax.all_to_all(send, 'ep', 0, 0, tiled=True)
        x = recv.reshape(G, el, cap, d).transpose(1, 0, 2, 3).reshape(el, G * cap, d)
        y = _experts(x, ue1, ue3, ue2)
        y = y.reshape(el, G, cap, d).transpose(1, 0, 2, 3).reshape(e, cap, d)
        back = lax.all_to_all(y, 'ep', 0, 0, tiled=True)
        yg = back[ix, sl]
        m = jnp.sum(g[..., None] * yg.astype(f32), axis=1)
        dense = _dense(h0, na, wq, wk, wv, wo, nf, w1, w3, w2)
        return (dense + m).astype(jnp.bfloat16).reshape(b, s, d)

    rows_spec = P(('dp', 'ep'))
    in_specs = (rows_spec,) * 3 + (P(),) * 11 + (P('ep'),) * 3
    return jax.shard_map(local, mesh=mesh, in_specs=in_specs, out_specs=rows_spec, check_vma=False)
```

profile of v0, /device:TPU:21, one launch (start us, length us, event | category | flops | bytes accessed | tf_op | source)
XLA Modules:
  0.0 533.1 jit_solution(12805911853118694932)
XLA Ops:
  0.0 0.9 shift-left_or_fusion
  0.9 0.7 and_reduce_fusion
  1.6 0.7 multiply_reduce_fusion.1
  2.3 0.1 copy.50
  2.4 0.1 reshape.356
  2.6 4.3 scatter_custom_fusion
  7.0 1.2 fusion.15
  8.2 0.7 convert_element_type.133
  8.9 0.1 copy.51
  9.0 0.1 copy.52
  9.2 1.2 fusion.21
  10.5 11.0 %gather_fusion = bf16[2048,2048]{1,0:T(8,128)(2,1)} fusion(bf16[128,2048]{1,0:T(8,128)(2,1)S(1)} %fusion.21, s32[2048]{0:T(1024)S(1)} %broadcast_clamp_fusion), kind=kCustom, calls=%fused_computation | custom fusion | bytes 16785408 | tf_op jit(solution)/shard_map/jit(_take)/gather | solution.py:81
  21.5 7.3 %broadcast_select_fusion = bf16[128,16,2048]{2,1,0:T(8,128)(2,1)} fusion(bf16[128,16,2048]{2,1,0:T(8,128)(2,1)} %bitcast.116, pred[128,16]{1,0:T(8,128)(4,1)S(1)} %copy.51), kind=kLoop, calls=%fused_computation.6 | loop fusion | flops 4194304 | bytes 16779264 | tf_op jit(solution)/shard_map/jit(_take)/select_n | solution.py:81
  28.8 195.9 %all_to_all.10 = bf16[128,16,2048]{2,1,0:T(8,128)(2,1)} all-to-all(bf16[128,16,2048]{2,1,0:T(8,128)(2,1)} %broadcast_select_fusion), channel_id=1, replica_groups=mesh['dp'=4,'ep'=16] {'ep'}, dimensions={0} | all-to-all | bytes 16777216 | tf_op jit(solution)/shard_map/all_to_all | solution.py:82
  224.7 8.3 %copy.53 = bf16[8,16,16,2048]{3,2,1,0:T(8,128)(2,1)} copy(bf16[8,16,16,2048]{3,2,0,1:T(8,128)(2,1)} %bitcast.115) | data formatting | bytes 16777216 | tf_op jit(solution)/shard_map/transpose | solution.py:83
  233.0 18.0 %fusion.48 = f32[8,256,768]{2,1,0:T(8,128)} fusion(bf16[8,256,2048]{2,1,0:T(8,128)(2,1)} %bitcast.118, bf16[8,2048,768]{2,1,0:T(8,128)(2,1)} %param.31), kind=kOutput, calls=%fused_computation.91 | convolution fusion | flops 6442450944 | bytes 39845888 | tf_op jit(solution)/shard_map/ecd,edf->ecf/dot_general | solution.py:59
  251.0 25.9 %convolution_convert_fusion = bf16[8,256,2048]{2,1,0:T(8,128)(2,1)} fusion(bf16[8,768,2048]{2,1,0:T(8,128)(2,1)} %param.33, f32[8,256,768]{2,1,0:T(8,128)} %fusion.48, bf16[8,256,2048]{2,1,0:T(8,128)(2,1)} %bitcast.119, bf16[8,2048,768]{2,1,0:T(8,128)(2,1)} %param.32), kind=kOutput, calls=%fused_computation.10 | convolution fusion | flops 12898533376 | bytes 73400320 | tf_op jit(solution)/shard_map/ecf,efd->ecd/dot_general | solution.py:62
  276.9 8.3 %copy.54 = bf16[16,8,16,2048]{3,2,1,0:T(8,128)(2,1)} copy(bf16[16,8,16,2048]{3,2,0,1:T(8,128)(2,1)} %bitcast.120) | data formatting | bytes 16777216 | tf_op jit(solution)/shard_map/transpose | solution.py:85
  285.2 5.2 all-to-all-start.1
  290.4 0.1 copy.48
  290.5 0.1 copy.49
  290.6 0.1 reshape.350
  290.7 0.1 copy.55
  290.8 0.1 reshape.344
  290.9 0.5 convolution_convert_fusion.2
  291.4 0.1 copy.59
  291.6 1.3 fusion.47
  292.9 6.8 %gather_fusion.2 = f32[1024]{0:T(1024)S(1)} fusion(f32[128,128]{1,0:T(8,128)S(1)} %fusion.47, s32[1024]{0:T(1024)S(1)} %reshape.350), kind=kCustom, calls=%fused_computation.2 | custom fusion | bytes 16384 | tf_op jit(solution)/shard_map/jit(take_along_axis)/gather | solution.py:53
  299.8 2.9 copy.60
  302.7 22.6 %copy.63 = bf16[4096,2048]{1,0:T(8,128)(2,1)} copy(bf16[4096,2048]{0,1:T(8,128)(2,1)} %bitcast.117) | data formatting | bytes 33554432 | tf_op jit(solution)/shard_map/dot_general | solution.py:33
  325.3 0.2 multiply_cosine_fusion
  325.5 8.4 %convolution_bitcast_fusion = f32[1,128,32,128]{1,3,2,0:T(8,128)S(1)} fusion(bf16[32,128,2048]{2,1,0:T(8,128)(2,1)} %bitcast.113, bf16[1,128,2048]{2,1,0:T(8,128)(2,1)S(1)} %copy-done.2, f32[2048]{0:T(1024)S(1)} %convert_element_type.119, f32[128]{0:T(128)S(1)} %add_rsqrt_fusion.1), kind=kOutput, calls=%fused_computation.23 | convolution fusion | flops 2148532224 | bytes 19407360 | tf_op jit(solution)/shard_map/dot_general | solution.py:33
  333.9 1.1 subtract_convert_fusion
  335.0 2.4 copy.44
  337.4 1.4 copy.43
  338.8 0.1 fusion.42
  338.9 0.2 fusion.36
  339.1 0.8 convolution_bitcast_fusion.1
  340.0 2.5 fusion.46
  342.4 0.4 fusion.8
  342.8 0.6 convolution_convert_fusion.1
  343.4 8.2 %multiply_reduce_fusion = (f32[128]{0:T(128)S(1)}, f32[128,2048]{1,0:T(8,128)S(1)}) fusion(bf16[128,4096]{0,1:T(8,128)(2,1)S(1)} %bitcast.125, bf16[4096,2048]{1,0:T(8,128)(2,1)} %param.24, bf16[1,128,2048]{2,1,0:T(8,128)(2,1)S(1)} %copy-done.2), kind=kOutput, calls=%fused_computation.41 | convolution fusion | flops 2149056512 | bytes 19399168 | tf_op jit(solution)/shard_map/dot_general | solution.py:42
  351.7 0.1 fusion.35
  351.8 13.6 %fusion.20 = f32[128,6144]{1,0:T(8,128)} fusion(bf16[2048,6144]{1,0:T(8,128)(2,1)} %param.26, f32[128,2048]{1,0:T(8,128)S(1)} %get-tuple-element.18, f32[2048]{0:T(1024)S(1)} %convert_element_type.130, f32[128]{0:T(128)S(1)} %add_rsqrt_fusion), kind=kOutput, calls=%fused_computation.44 | convolution fusion | flops 3222011904 | bytes 29368832 | tf_op jit(solution)/shard_map/dot_general | solution.py:44
  365.4 114.0 %all-to-all-done.1 = bf16[128,16,2048]{2,1,0:T(8,128)(2,1)} async-done(((bf16[128,16,2048]{2,1,0:T(8,128)(2,1)}), bf16[128,16,2048]{2,1,0:T(8,128)(2,1)}, u32[]{:S(2)}, u32[]{:S(2)}) %all-to-all-start.1) | async-done | bytes 8388640 | tf_op jit(solution)/shard_map/all_to_all | solution.py:86
  479.4 25.5 %gather_fusion.1 = bf16[1024,2048]{1,0:T(8,128)(2,1)} fusion(bf16[128,16,2048]{2,1,0:T(8,128)(2,1)} %all-to-all-done.1, s32[1024]{0:T(1024)S(1)} %reshape.344), kind=kCustom, calls=%fused_computation.1 | custom fusion | bytes 8396800 | tf_op jit(solution)/shard_map/gather | solution.py:87
  504.9 7.5 %fusion = f32[128,2048]{1,0:T(8,128)} fusion(bf16[1024,2048]{1,0:T(8,128)(2,1)} %gather_fusion.1, f32[128,8]{1,0:T(8,128)S(1)} %fusion.35), kind=kLoop, calls=%fused_computation.5 | loop fusion | flops 6029312 | bytes 5246976 | tf_op jit(solution)/shard_map/reduce_sum | solution.py:88
  512.4 20.6 %fusion.7 = bf16[1,128,2048]{2,1,0:T(8,128)(2,1)} fusion(f32[128,2048]{1,0:T(8,128)} %fusion, f32[128,2048]{1,0:T(8,128)S(1)} %copy-done.4, bf16[6144,2048]{1,0:T(8,128)(2,1)} %param.28, bf16[2048,6144]{1,0:T(8,128)(2,1)} %param.27, f32[128,6144]{1,0:T(8,128)} %fusion.20, f32[2048]{0:T(1024)S(1)} %convert_element_type.130, f32[128]{0:T(128)S(1)} %add_rsqrt_fusion), kind=kOutput, calls=%fused_computation.18 | convolution fusion | flops 6448742400 | bytes 56107520 | tf_op jit(solution)/shard_map/dot_general | solution.py:45
  (32 shorter events, 0.4 us)
Async XLA Ops:
  0.0 290.9 %copy-start = (bf16[2048,512]{1,0:T(8,128)(2,1)S(1)}, bf16[2048,512]{1,0:T(8,128)(2,1)}, u32[]{:S(2)}) copy-start(bf16[2048,512]{1,0:T(8,128)(2,1)} %param.23) | copy-start | bytes 6291460
  285.2 5.2 copy-start.5
  285.2 5.3 copy-start.6
  285.2 5.3 %copy-start.7 = (bf16[2048]{0:T(1024)(128)(2,1)S(1)}, bf16[2048]{0:T(1024)(128)(2,1)}, u32[]{:S(2)}) copy-start(bf16[2048]{0:T(1024)(128)(2,1)} %param.25) | copy-start | bytes 12292
  285.2 5.8 %copy-start.2 = (bf16[1,128,2048]{2,1,0:T(8,128)(2,1)S(1)}, bf16[1,128,2048]{2,1,0:T(8,128)(2,1)}, u32[]{:S(2)}) copy-start(bf16[1,128,2048]{2,1,0:T(8,128)(2,1)} %param.17) | copy-start | bytes 1572868
  285.2 194.2 %all-to-all-start.1 = ((bf16[128,16,2048]{2,1,0:T(8,128)(2,1)}), bf16[128,16,2048]{2,1,0:T(8,128)(2,1)}, u32[]{:S(2)}, u32[]{:S(2)}) async-start(bf16[128,16,2048]{2,1,0:T(8,128)(2,1)} %bitcast.114), calls=%async_computation.1 | async-start | bytes 16777216 | tf_op jit(solution)/shard_map/all_to_all | solution.py:86
  351.7 13.7 %copy-start.3 = (f32[128,2048]{1,0:T(8,128)}, f32[128,2048]{1,0:T(8,128)S(1)}, u32[]{:S(2)}) copy-start(f32[128,2048]{1,0:T(8,128)S(1)} %get-tuple-element.18) | copy-start | bytes 3145732
  479.4 33.0 %copy-start.4 = (f32[128,2048]{1,0:T(8,128)S(1)}, f32[128,2048]{1,0:T(8,128)}, u32[]{:S(2)}) copy-start(f32[128,2048]{1,0:T(8,128)} %copy-done.3) | copy-start | bytes 3145732
  512.4 20.6 %copy-start.1 = (bf16[2048,512]{1,0:T(8,128)(2,1)S(1)}, bf16[2048,512]{1,0:T(8,128)(2,1)}, u32[]{:S(2)}) copy-start(bf16[2048,512]{1,0:T(8,128)(2,1)} %param.23) | copy-start | bytes 6291460
where the time goes:
time: 535 us; the launch traced here: 533 us
  blocking collectives  196 us (37%)
  waiting for transfers between devices  114 us (21%)
  matrix products  101 us (19%)
  local copies, waits for them, and re-layouts  94.7 us (18%)
  other arithmetic  22.5 us (4%)
    all_to_all x1, blocking collectives, local(): recv = lax.all_to_all(send, 'ep', 0, 0, tiled=True)  196 us
    all_to_all x1, waiting for transfers between devices, local(): back = lax.all_to_all(y, 'ep', 0, 0, tiled=True)  114 us
    dot_general x1, matrix products, _experts(): jnp.einsum('ecf,efd->ecd', hid, ue2, preferred_element_type=f32)  25.9 us
    gather x1, local copies, waits for them, and re-layouts, local(): yg = back[ix, sl]  25.5 us
    dot_general x1, local copies, waits for them, and re-layouts, _dense(): jnp.dot(x, wq, preferred_element_type=f32).reshape(b, s, nh, HEAD)  22.6 us
    dot_general x1, matrix products, _dense(): return a.astype(f32) + jnp.dot(hid, w2, preferred_element_type=f32)  20.6 us
    dot_general x1, matrix products, _experts(): h1 = jnp.einsum('ecd,edf->ecf', x, ue1, preferred_element_type=f32)  18 us
    dot_general x1, matrix products, _dense(): jnp.dot(z, w1, preferred_element_type=f32)  13.6 us
  transfers between devices with their start and end apart: 1, of which 1 were waited for; matrix products, arithmetic and copies ran while one was open for 14% of the time, Pallas kernels for 0%

commit v1 on v0

v1 whole, which is shorter than its diff:
```python
import functools

import jax
import jax.numpy as jnp
import numpy as np
from jax import lax
from jax.experimental import pallas as pl
from jax.experimental.pallas import tpu as pltpu
from jax.sharding import PartitionSpec as P

HEAD = 128
EPS = 1e-6
ROPE_BASE = 10000.0
TN = 256
NS = 4
VMEM_LIMIT = 66_500_000
MESH = pl.DeviceIdType.MESH
F32, BF = jnp.float32, jnp.bfloat16


def _rms_rows(xf, w):
    r = lax.rsqrt(jnp.mean(xf * xf, axis=-1, keepdims=True) + EPS)
    return (xf * r * w).astype(BF)


def _silu(x):
    return x * jax.nn.sigmoid(x)


def _div(x, n):
    return x // n if isinstance(x, int) else lax.div(x, n)


def _rem(x, n):
    return x % n if isinstance(x, int) else lax.rem(x, n)


def _dot(a, b):
    return jnp.dot(a, b, preferred_element_type=F32)


class Phase:
    def __init__(self, n, copies):
        self.n, self.copies, self.start = n, copies, 0


def _kernel(Z, T, D, NQ, NK, FF, EL, FE, CAP,
            h0, keyt, idxt, na, nf, nm, wr, cosr, sinr,
            wq, wk, wv, wo, w1, w3, w2, ue1, ue3, ue2,
            out,
            ubuf, kg, x, hid, ys, yr, g3, rb, ms, mr, wbuf, xn, qkv, o, a, fh, f,
            wsem, own_s, own_r, ag_s, ag_r, kg_s, kg_r, dd_s, dd_r, y_s, y_r, rs_s, rs_r, m_s, m_r):
    ep = lax.axis_index("ep")
    z = _div(ep, 2)
    k = _rem(ep, 2)
    ok = 1 - k
    RC = T // 16
    HC = RC // 2
    NC = D // TN
    NCH = NC // 2
    NM = 4 * HC - 2 if Z == 8 else None
    assert Z == 8 and HC == 4 and NCH == 4
    NSL = EL * CAP

    def dev(zz, kk):
        return {"ep": zz * 2 + kk}

    right, left = _rem(z + 1, Z), _rem(z + Z - 1, Z)
    nbr = (right, left)

    def rcopy(src, dst, s, r, zz, kk):
        return pltpu.make_async_remote_copy(src_ref=src, dst_ref=dst, send_sem=s, recv_sem=r,
                                            device_id=dev(zz, kk), device_id_type=MESH)

    def cols(i):
        return pl.ds(i * TN if isinstance(i, int) else pl.multiple_of(i * TN, TN), TN)

    def wslot(slot, lo, n):
        return wbuf.at[slot, pl.ds(lo, n)]

    nq2, nk2 = NQ // (2 * TN), NK // (2 * TN)

    def qkv_copies(i, slot):
        res = []
        for h in range(2):
            for cond, src, off in ((i < nq2, wq, 0), ((i >= nq2) & (i < nq2 + nk2), wk, nq2),
                                   (i >= nq2 + nk2, wv, nq2 + nk2)):
                res.append((cond, lambda src=src, off=off, h=h: pltpu.make_async_copy(
                    src.at[:, cols(2 * (i - off) + h)], wslot(slot, h * D, D), wsem.at[slot, h])))
        return res

    def wo_copies(i, slot):
        return [(None, lambda: pltpu.make_async_copy(wo.at[:, cols(i)], wslot(slot, 0, NQ), wsem.at[slot, 0]))]

    def w13_copies(i0):
        def go(i, slot):
            return [(None, lambda: pltpu.make_async_copy(w1.at[:, cols(i + i0)], wslot(slot, 0, D), wsem.at[slot, 0])),
                    (None, lambda: pltpu.make_async_copy(w3.at[:, cols(i + i0)], wslot(slot, D, D), wsem.at[slot, 1]))]
        return go

    def w2_copies(i, slot):
        return [(None, lambda: pltpu.make_async_copy(w2.at[:, cols(i)], wslot(slot, 0, FF), wsem.at[slot, 0]))]

    NJ = FE // TN

    def e1_copies(i, slot):
        e, j = _div(i, NJ), _rem(i, NJ)
        return [(None, lambda: pltpu.make_async_copy(ue1.at[e, :, cols(j)], wslot(slot, 0, D), wsem.at[slot, 0])),
                (None, lambda: pltpu.make_async_copy(ue3.at[e, :, cols(j)], wslot(slot, D, D), wsem.at[slot, 1]))]

    def e2_col(i):
        q = _div(i, 2)
        c = _rem(q, 2) * 2 + _div(q, 2)
        half = jnp.where(_rem(i, 2) == 0, ok, k)
        return half, c

    def e2_copies(i, slot):
        half, c = e2_col(i)
        return [(None, lambda e=e: pltpu.make_async_copy(
            ue2.at[e, :, cols(half * NCH + c)], wslot(slot, e * FE, FE), wsem.at[slot, e])) for e in range(EL)]

    n13 = FF // TN
    n13a = n13 // 4
    ph_qkv = Phase(nq2 + 2 * nk2, qkv_copies)
    ph_wo = Phase(D // TN, wo_copies)
    ph_13a = Phase(n13a, w13_copies(0))
    ph_e1 = [Phase(EL * NJ, e1_copies), Phase(EL * NJ, e1_copies)]
    ph_e2 = [Phase(NC, e2_copies), Phase(NC, e2_copies)]
    ph_13b = Phase(n13 - n13a, w13_copies(n13a))
    ph_2 = Phase(D // TN, w2_copies)
    order = [ph_qkv, ph_wo, ph_13a, ph_e1[0], ph_e2[0], ph_e1[1], ph_e2[1], ph_13b, ph_2]
    total = 0
    for q, ph in enumerate(order):
        ph.start, ph.pos = total, q
        total += ph.n

    def do(copies, act):
        for cond, mk in copies:
            if cond is None:
                act(mk())
            else:
                pl.when(cond)(lambda mk=mk: act(mk()))

    def issue(t, phases):
        slot = _rem(t, NS)
        for ph in phases:
            def go(ph=ph):
                do(ph.copies(t - ph.start, slot), lambda c: c.start())
            pl.when((t >= ph.start) & (t < ph.start + ph.n))(go)

    def run(ph, body, events=None):
        nxt = order[ph.pos:ph.pos + 2]

        def it(i, _):
            t = ph.start + i
            slot = _rem(t, NS)
            do(ph.copies(i, slot), lambda c: c.wait())
            body(i, slot)
            issue(t + NS, nxt)
            if events is not None:
                events(i)
            return 0

        lax.fori_loop(0, ph.n, it, 0)

    def at(i, start, stride, count, fn, e0):
        n = _div(i - start, stride)
        pl.when((i >= start) & (_rem(i - start, stride) == 0) & (n < count))(lambda: fn(e0 + n))

    def ag_desc(p, dirn, i):
        d = _div(i, 4)
        c = _rem(i + 2 * dirn, 4)
        org = _rem(z - d + Z, Z) if dirn == 0 else _rem(z + d, Z)
        blk = ubuf.at[p, org, k * HC + c]
        return rcopy(blk, blk, ag_s.at[p, dirn, i], ag_r.at[p, dirn, i], nbr[dirn], k)

    def kg_desc(p, dirn, d):
        org = _rem(z - d + Z, Z) if dirn == 0 else _rem(z + d, Z)
        blk = kg.at[p, org]
        return rcopy(blk, blk, kg_s.at[p, dirn, d], kg_r.at[p, dirn, d], nbr[dirn], k)

    def dd_desc(p, dirn, i):
        d = _div(i, 4) + 1
        c = _rem(i + 2 * dirn, 4)
        org = _rem(z - d + Z, Z) if dirn == 0 else _rem(z + d, Z)
        blk = ubuf.at[p, org, k * HC + c]
        return rcopy(blk, blk, dd_s.at[p, dirn, i], dd_r.at[p, dirn, i], z, ok)

    def own_descs(p):
        return (rcopy(ubuf.at[p, z], ubuf.at[p, z], own_s.at[0], own_r.at[0], z, ok),
                rcopy(kg.at[p, z], kg.at[p, z], own_s.at[1], own_r.at[1], z, ok))

    NKG = (4, 3)

    def ag_begin(p):
        @pl.when(k != p)
        def _():
            for c in own_descs(p):
                c.wait_recv()
        for i in range(4):
            for dirn in range(2):
                ag_desc(p, dirn, i).start()
                if i == 0:
                    kg_desc(p, dirn, 0).start()

    def ag_event(p):
        def ev(i):
            for dirn in range(2):
                ag_desc(p, dirn, i).wait_recv()
                pl.when(i < 10)(lambda: ag_desc(p, dirn, i + 4).start())
                dd_desc(p, dirn, i).start()
                q = _div(i, 4)

                @pl.when((_rem(i, 4) == 0) & (q < NKG[dirn]))
                def _():
                    kg_desc(p, dirn, q).wait_recv()
                    pl.when(q + 1 < NKG[dirn])(lambda: kg_desc(p, dirn, q + 1).start())
        return ev

    def ag_drain(p):
        for dirn in range(2):
            @pl.loop(0, 14)
            def _(i):
                dd_desc(p, dirn, i).wait_recv()

    def key_hits(p, zs, j, base, n):
        keys = kg[p, zs, j:j + 1, :].astype(jnp.int32)
        return keys == base + lax.broadcasted_iota(jnp.int32, (n, T), 0)

    def select(p, zs):
        base = ep * NSL
        s = jnp.zeros((NSL, T), jnp.bool_)
        s = key_hits(p, zs, 0, base, NSL)
        for j in range(1, 8):
            s = s | key_hits(p, zs, j, base, NSL)
        s = jnp.where(s, 1.0, 0.0).astype(BF)
        for n in range(D // 512):
            u = ubuf[p, zs, :, :, n * 512:(n + 1) * 512].reshape(T, 512)
            xs = _dot(s, u).astype(BF)
            for e in range(EL):
                x[e, zs, :, n * 512:(n + 1) * 512] = xs[e * CAP:(e + 1) * CAP]

    def gates(p, zs):
        parts = []
        for kk in (k, ok):
            base = (z * 2 + kk) * NSL
            gt = jnp.zeros((NSL, T), F32)
            for j in range(8):
                gt = gt + jnp.where(key_hits(p, zs, j, base, NSL), kg[p, zs, 8 + j:9 + j, :], 0.0)
            parts.append(gt.T)
        for h, gt in enumerate(parts):
            hi = gt.astype(BF)
            r = gt - hi.astype(F32)
            mid = r.astype(BF)
            lo = (r - mid.astype(F32)).astype(BF)
            for q, v in enumerate((hi, mid, lo)):
                g3[p, zs, q * T:(q + 1) * T, h * NSL:(h + 1) * NSL] = v

    def combine(p, zd, c):
        yy = jnp.concatenate([ys[p, k, c, zd], yr[p, c, zd]], axis=0)
        r = _dot(g3[p, zd], yy)
        return r[:T] + (r[T:2 * T] + r[2 * T:])

    def rs_desc(p, dirn, i):
        return rcopy(rb.at[p, dirn, i], rb.at[p, dirn, i + 4], rs_s.at[p, dirn, i], rs_r.at[p, dirn, i],
                     nbr[dirn], k)

    def rs_event(p):
        def ev(i):
            j = i + 2
            d = 4 - _div(j, 4)
            for dirn in range(2):
                c = _rem(j + 2 - 2 * dirn, 4)
                zd = _rem(z + d, Z) if dirn == 0 else _rem(z - d + Z, Z)
                part = combine(p, zd, c)

                @pl.when(i >= 4)
                def _():
                    rs_desc(p, dirn, i - 4).wait_recv()
                    rb[p, dirn, i] = rb[p, dirn, i] + part

                @pl.when(i < 4)
                def _():
                    rb[p, dirn, i] = part
            for dirn in range(2):
                rs_desc(p, dirn, i).start()
        return ev

    def m_desc(p):
        return rcopy(ms.at[p], mr, m_s.at[0], m_r.at[0], z, ok)

    def rs_final(p):
        @pl.loop(0, 4)
        def _(s):
            c = _rem(s + 2, 4)
            rs_desc(p, 0, 10 + s).wait_recv()
            ms[p, c] = combine(p, z, c) + rb[p, 0, 14 + s]

        @pl.loop(0, 4)
        def _(c):
            rs_desc(p, 1, 10 + c).wait_recv()
            ms[p, c] = ms[p, c] + rb[p, 1, 14 + c]

        pl.when(k != p)(lambda: m_desc(p).start())

    def y_desc(p, c):
        return rcopy(ys.at[p, ok, c], yr.at[p, c], y_s.at[p, c], y_r.at[p, c], z, ok)

    def qkv_body(i, slot):
        last = i >= nq2 + nk2
        cs = jnp.where(last, 1.0, cosr[...])
        sn = jnp.where(last, 0.0, sinr[...])
        for h in range(2):
            r = _dot(xn[...], wbuf[slot, h * D:(h + 1) * D])
            parts = []
            for b in range(TN // HEAD):
                v = r[:, b * HEAD:(b + 1) * HEAD]
                parts.append(v * cs + pltpu.roll(v, HEAD // 2, 1) * sn)
            qkv[:, cols(2 * i + h)] = jnp.concatenate(parts, axis=1).astype(BF)

    nkv = NK // HEAD
    rep = NQ // NK

    def attn(g):
        def hd(i):
            return pl.ds(pl.multiple_of(i * HEAD, HEAD), HEAD)
        kk = qkv[:, hd(NQ // HEAD + g)]
        vv = qkv[:, hd(NQ // HEAD + nkv + g)]
        causal = lax.broadcasted_iota(jnp.int32, (T, T), 0) >= lax.broadcasted_iota(jnp.int32, (T, T), 1)
        for hh in range(rep):
            qh = qkv[:, hd(g * rep + hh)]
            s = lax.dot_general(qh, kk, (((1,), (1,)), ((), ())), preferred_element_type=F32) * HEAD ** -0.5
            s = jnp.where(causal, s, -jnp.inf)
            e = jnp.exp(s - jnp.max(s, axis=-1, keepdims=True))
            pr = (e / jnp.sum(e, axis=-1, keepdims=True)).astype(BF)
            o[:, hd(g * rep + hh)] = _dot(pr, vv).astype(BF)

    def wo_body(i, slot):
        r = _dot(o[...], wbuf[slot, :NQ])
        a[:, cols(i)] = (h0[:, cols(i)].astype(F32) + r).astype(BF)

    def w13_body(i0):
        def body(i, slot):
            h1 = _dot(xn[...], wbuf[slot, :D])
            h3 = _dot(xn[...], wbuf[slot, D:2 * D])
            fh[:, cols(i + i0)] = (_silu(h1) * h3).astype(BF)
        return body

    def w2_body(i, slot):
        f[:, cols(i)] = _dot(fh[...], wbuf[slot, :FF])

    def e1_body(i, slot):
        e, j = _div(i, NJ), _rem(i, NJ)
        xe = x[e].reshape(Z * CAP, D)
        h1 = _dot(xe, wbuf[slot, :D])
        h3 = _dot(xe, wbuf[slot, D:2 * D])
        hid[e, :, cols(j)] = (_silu(h1) * h3).astype(BF)

    def e2_body(p):
        def body(i, slot):
            half, c = e2_col(i)
            for e in range(EL):
                r = _dot(hid[e], wbuf[slot, e * FE:(e + 1) * FE]).astype(BF)
                for zs in range(Z):
                    ys[p, half, c, zs, e * CAP:(e + 1) * CAP, :] = r[zs * CAP:(zs + 1) * CAP]
            pl.when(_rem(i, 2) == 0)(lambda: y_desc(p, c).start())
        return body

    barrier = pltpu.get_barrier_semaphore()
    for zz, kk in ((right, k), (left, k), (z, ok)):
        pl.semaphore_signal(barrier, inc=1, device_id=dev(zz, kk), device_id_type=MESH)

    for t in range(NS):
        issue(t, [ph_qkv])

    @pl.loop(0, RC)
    def _(r):
        rows = pl.ds(pl.multiple_of(r * 16, 16), 16)
        hf = h0[rows, :].astype(F32)
        ubuf[k, z, r] = _rms_rows(hf, nm[...].astype(F32))
        xn[rows, :] = _rms_rows(hf, na[...].astype(F32))

    lt = _dot(ubuf[k, z].reshape(T, D), wr[...]).T
    rows = []
    for j in range(8):
        hit = lax.broadcasted_iota(jnp.int32, lt.shape, 0) == idxt[j:j + 1, :]
        rows.append(jnp.sum(jnp.where(hit, lt, 0.0), axis=0, keepdims=True))
    sel = jnp.concatenate(rows, axis=0)
    ex = jnp.exp(sel - jnp.max(sel, axis=0, keepdims=True))
    kg[k, z, 0:8, :] = keyt[...].astype(F32)
    kg[k, z, 8:16, :] = ex / jnp.sum(ex, axis=0, keepdims=True)

    pl.semaphore_wait(barrier, 3)
    for p in range(2):
        @pl.when(k == p)
        def _():
            for c in own_descs(p):
                c.start()
    ag_begin(0)

    ag0, ag1 = ag_event(0), ag_event(1)
    rs0, rs1 = rs_event(0), rs_event(1)

    run(ph_qkv, qkv_body, lambda i: at(i, 3, 2, 3, ag0, 0))

    @pl.loop(0, nkv)
    def _(g):
        attn(g)
        ag0(3 + g)

    run(ph_wo, wo_body, lambda i: at(i, 1, 2, 4, ag0, 7))
    ag_begin(1)

    @pl.loop(0, RC)
    def _(r):
        rows = pl.ds(pl.multiple_of(r * 16, 16), 16)
        xn[rows, :] = _rms_rows(a[rows, :].astype(F32), nf[...].astype(F32))

    run(ph_13a, w13_body(0), lambda i: at(i, 1, 2, 3, ag0, 11))
    ag_drain(0)

    @pl.loop(0, Z)
    def _(zs):
        select(0, zs)

    run(ph_e1[0], e1_body, lambda i: at(i, 0, 2, 12, ag1, 0))

    @pl.loop(0, Z)
    def _(zs):
        gates(0, zs)

    run(ph_e2[0], e2_body(0), lambda i: at(i, 0, 2, 2, ag1, 12))
    for c in range(4):
        y_desc(0, c).wait_recv()

    @pl.loop(0, 4)
    def _(i):
        rs0(i)

    ag_drain(1)

    @pl.loop(0, Z)
    def _(zs):
        select(1, zs)
        gates(1, zs)

    run(ph_e1[1], e1_body, lambda i: at(i, 1, 4, 6, rs0, 4))
    run(ph_e2[1], e2_body(1), lambda i: at(i, 2, 3, 2, rs0, 10))
    for c in range(4):
        y_desc(1, c).wait_recv()

    @pl.loop(12, 14)
    def _(i):
        rs0(i)

    @pl.loop(0, 4)
    def _(i):
        rs1(i)

    run(ph_13b, w13_body(n13a))
    rs_final(0)
    run(ph_2, w2_body, lambda i: at(i, 0, 2, 4, rs1, 4))

    @pl.loop(8, 14)
    def _(i):
        rs1(i)

    rs_final(1)
    pl.when(k == 0)(lambda: m_desc(0).wait_recv())
    pl.when(k == 1)(lambda: m_desc(1).wait_recv())

    @pl.loop(0, 4)
    def _(c):
        own = cols(k * NCH + c)
        out[:, own] = (a[:, own].astype(F32) + f[:, own] + ms[k, c]).astype(BF)
        oth = cols(ok * NCH + c)
        out[:, oth] = (a[:, oth].astype(F32) + f[:, oth] + mr[c]).astype(BF)

    for p in range(2):
        @pl.when(k == p)
        def _():
            for c in own_descs(p):
                c.wait_send()
        pl.when(k != p)(lambda: m_desc(p).wait_send())
        for dirn in range(2):
            @pl.loop(0, 14)
            def _(i):
                ag_desc(p, dirn, i).wait_send()
                dd_desc(p, dirn, i).wait_send()
                rs_desc(p, dirn, i).wait_send()

            @pl.loop(0, NKG[dirn])
            def _(d):
                kg_desc(p, dirn, d).wait_send()

        @pl.loop(0, 4)
        def _(c):
            y_desc(p, c).wait_send()


def solution(mesh):
    G = mesh.shape['ep']

    def local(h0, idx, slot, na, wq, wk, wv, wo, nf, w1, w3, w2, nm, wr, ue1, ue3, ue2):
        b, s, d = h0.shape
        t = b * s
        kt = idx.shape[-1]
        el = ue1.shape[0]
        e = el * G
        cap = 2 * t * kt // e
        Z = G // 2
        nq, nk, ff, fe = wq.shape[1], wk.shape[1], w1.shape[1], ue1.shape[2]
        keyt = (idx * cap + slot).reshape(t, kt).T
        idxt = idx.reshape(t, kt).T
        pos = np.arange(s, dtype=np.float64)
        inv = ROPE_BASE ** (-2.0 * np.arange(HEAD // 2, dtype=np.float64) / HEAD)
        ang = pos[:, None] * inv[None, :]
        cosr = np.concatenate([np.cos(ang), np.cos(ang)], axis=1).astype(np.float32)
        sinr = np.concatenate([-np.sin(ang), np.sin(ang)], axis=1).astype(np.float32)
        nslot = el * cap
        rows = max(2 * d, nq, ff, el * fe)
        vm = pl.BlockSpec(memory_space=pltpu.VMEM)
        hb = pl.BlockSpec(memory_space=pl.ANY)
        V, DMA = pltpu.VMEM, pltpu.SemaphoreType.DMA
        kern = functools.partial(_kernel, Z, t, d, nq, nk, ff, el, fe, cap)
        out = pl.pallas_call(
            kern,
            out_shape=jax.ShapeDtypeStruct((t, d), BF),
            in_specs=[vm] * 9 + [hb] * 10,
            out_specs=vm,
            scratch_shapes=[
                V((2, Z, t // 16, 16, d), BF),
                V((2, Z, 16, t), F32),
                V((el, Z, cap, d), BF),
                V((el, Z * cap, fe), BF),
                V((2, 2, 4, Z, nslot, TN), BF),
                V((2, 4, Z, nslot, TN), BF),
                V((2, Z, 3 * t, 2 * nslot), BF),
                V((2, 2, 18, t, TN), F32),
                V((2, 4, t, TN), F32),
                V((4, t, TN), F32),
                V((NS, rows, TN), BF),
                V((t, d), BF),
                V((t, nq + 2 * nk), BF),
                V((t, nq), BF),
                V((t, d), BF),
                V((t, ff), BF),
                V((t, d), F32),
                DMA((NS, 8)),
                DMA((2,)), DMA((2,)),
                DMA((2, 2, 14)), DMA((2, 2, 14)),
                DMA((2, 2, 4)), DMA((2, 2, 4)),
                DMA((2, 2, 14)), DMA((2, 2, 14)),
                DMA((2, 4)), DMA((2, 4)),
                DMA((2, 2, 14)), DMA((2, 2, 14)),
                DMA((1,)), DMA((1,)),
            ],
            compiler_params=pltpu.CompilerParams(
                collective_id=0, has_side_effects=True, vmem_limit_bytes=VMEM_LIMIT),
            name="layer_pair",
        )(h0.reshape(t, d), keyt, idxt, na.reshape(1, d), nf.reshape(1, d), nm.reshape(1, d), wr,
          jnp.asarray(cosr), jnp.asarray(sinr), wq, wk, wv, wo, w1, w3, w2, ue1, ue3, ue2)
        return out.reshape(b, s, d)

    rows_spec = P(('dp', 'ep'))
    in_specs = (rows_spec,) * 3 + (P(),) * 11 + (P('ep'),) * 3
    return jax.shard_map(local, mesh=mesh, in_specs=in_specs, out_specs=rows_spec, check_vma=False)
```

time: 535 us -> 163 us (0.30)
  blocking collectives: 196 us -> 0 us
  Pallas kernels: 0 us -> 156 us
  waiting for transfers between devices: 114 us -> 0 us
  matrix products: 101 us -> 0 us
  local copies, waits for them, and re-layouts: 94.7 us -> 5.74 us
  other arithmetic: 22.5 us -> 1.3 us
    all_to_all x1 -> x0, blocking collectives: 196 us -> none  [local(): recv = lax.all_to_all(send, 'ep', 0, 0, tiled=True)]
    pallas_call x0 -> x1, Pallas kernels: none -> 156 us  [local(): pl.pallas_call(kern, out_shape=jax.ShapeDtypeStruct((t, d), BF), in_specs...]
    all_to_all x1 -> x0, waiting for transfers between devices: 114 us -> none  [local(): back = lax.all_to_all(y, 'ep', 0, 0, tiled=True)]
    dot_general x11 -> x0, matrix products: 101 us -> none  [the longest x1 25.9 us: _experts(): jnp.einsum('ecf,efd->ecd', hid, ue2, preferred_element_type=f32)]
    gather x6 -> x0, local copies, waits for them, and re-layouts: 43.6 us -> none  [the longest x1 25.5 us: local(): yg = back[ix, sl]]
    dot_general x2 -> x0, local copies, waits for them, and re-layouts: 25.5 us -> none  [the longest x1 22.6 us: _dense(): jnp.dot(x, wq, preferred_element_type=f32).reshape(b, s, nh, HEAD)]
    transpose x2 -> x0, local copies, waits for them, and re-layouts: 16.5 us -> none  [the longest x1 8.27 us: local(): recv.reshape(G, el, cap, d).transpose(1, 0, 2, 3).reshape(el, G * cap, d)]
    reduce_sum x4 -> x0, other arithmetic: 9.33 us -> none  [the longest x1 7.55 us: local(): m = jnp.sum(g[..., None] * yg.astype(f32), axis=1)]
  transfers between devices with their start and end apart: 1 -> 0, of which waited for: 1 -> 0; matrix products, arithmetic and copies ran while one was open for 14% -> 0% of each run, Pallas kernels for 0% -> 0%
where the time goes in v1:
time: 163 us
  Pallas kernels  156 us (96%)
  local copies, waits for them, and re-layouts  5.74 us (4%)
    pallas_call x1, Pallas kernels, local(): pl.pallas_call(kern, out_shape=jax.ShapeDtypeStruct((t, d), BF), in_specs...  156 us

profile of v1, /device:TPU:21, one launch (start us, length us, event | category | flops | bytes accessed | tf_op | source)
XLA Modules:
  0.0 162.9 jit_solution(2522072671180277748)
XLA Ops:
  0.0 1.3 add_bitcast_fusion.keyt
  1.3 1.3 reshape.24.na
  2.6 1.3 reshape.25.nf
  3.9 1.3 reshape.26.nm
  5.2 155.8 %layer_pair.1 = bf16[128,2048]{1,0:T(8,128)(2,1)} custom-call(bf16[128,2048]{1,0:T(8,128)(2,1)} %bitcast.10, s32[8,128]{1,0:T(8,128)} %add_bitcast_fusion.keyt, s32[8,128]{1,0:T(8,128)} %bitcast.11, bf16[1,2048]{1,0:T(2,128)(2,1)} %reshape.24.na, bf16[1,2048]{1,0:T(2,128)(2,1)} %reshape.25.nf, bf16[1,2048]{1,0:T(2,128)(2,1)} %reshape.26.nm, ...), custom_call_target="tpu_custom_call" | custom-call | tf_op jit(solution)/shard_map/layer_pair/pallas_call | solution.py:526
  161.0 1.9 %copy.21 = bf16[1,128,2048]{2,1,0:T(8,128)(2,1)} copy(bf16[1,128,2048]{2,1,0:T(8,128)(2,1)} %bitcast.9) | data formatting | bytes 1048576

commit v2 on v1

--- a/solution.py
+++ b/solution.py
@@ -45,11 +45,11 @@
 
 
 def _kernel(Z, T, D, NQ, NK, FF, EL, FE, CAP,
-            h0, keyt, idxt, na, nf, nm, wr, cosr, sinr,
+            h0, idx, slot, na, nf, nm, cosr, sinr, wr,
             wq, wk, wv, wo, w1, w3, w2, ue1, ue3, ue2,
             out,
-            ubuf, kg, x, hid, ys, yr, g3, rb, ms, mr, wbuf, xn, qkv, o, a, fh, f,
-            wsem, own_s, own_r, ag_s, ag_r, kg_s, kg_r, dd_s, dd_r, y_s, y_r, rs_s, rs_r, m_s, m_r):
+            ubuf, kg, x, hid, ys, yr, g3, rb, ms, mr, wbuf, xn, qkv, o, a, fh, f, wrv,
+            wsem, wr_sem, own_s, own_r, ag_s, ag_r, kg_s, kg_r, dd_s, dd_r, y_s, y_r, rs_s, rs_r, m_s, m_r):
     ep = lax.axis_index("ep")
     z = _div(ep, 2)
     k = _rem(ep, 2)
@@ -74,6 +74,9 @@
 
     def cols(i):
         return pl.ds(i * TN if isinstance(i, int) else pl.multiple_of(i * TN, TN), TN)
+
+    def row(w):
+        return w[...].astype(F32).reshape(1, D)
 
     def wslot(slot, lo, n):
         return wbuf.at[slot, pl.ds(lo, n)]
@@ -186,42 +189,58 @@
         blk = ubuf.at[p, org, k * HC + c]
         return rcopy(blk, blk, dd_s.at[p, dirn, i], dd_r.at[p, dirn, i], z, ok)
 
-    def own_descs(p):
-        return (rcopy(ubuf.at[p, z], ubuf.at[p, z], own_s.at[0], own_r.at[0], z, ok),
-                rcopy(kg.at[p, z], kg.at[p, z], own_s.at[1], own_r.at[1], z, ok))
+    def own_desc(p, q):
+        blk = (ubuf, kg)[q].at[p, z]
+        return rcopy(blk, blk, own_s.at[q], own_r.at[q], z, ok)
 
     NKG = (4, 3)
 
-    def ag_begin(p):
-        @pl.when(k != p)
-        def _():
-            for c in own_descs(p):
-                c.wait_recv()
+    def ag_send_own(p):
         for i in range(4):
             for dirn in range(2):
                 ag_desc(p, dirn, i).start()
-                if i == 0:
-                    kg_desc(p, dirn, 0).start()
+
+    def kg_send_own(p):
+        for dirn in range(2):
+            kg_desc(p, dirn, 0).start()
 
     def ag_event(p):
         def ev(i):
             for dirn in range(2):
                 ag_desc(p, dirn, i).wait_recv()
                 pl.when(i < 10)(lambda: ag_desc(p, dirn, i + 4).start())
+            for dirn in range(2):
                 dd_desc(p, dirn, i).start()
-                q = _div(i, 4)
-
-                @pl.when((_rem(i, 4) == 0) & (q < NKG[dirn]))
+            q = _div(i, 4)
+            for dirn in range(2):
+                @pl.when((_rem(i, 4) == 1) & (q < NKG[dirn]))
                 def _():
                     kg_desc(p, dirn, q).wait_recv()
                     pl.when(q + 1 < NKG[dirn])(lambda: kg_desc(p, dirn, q + 1).start())
         return ev
 
-    def ag_drain(p):
-        for dirn in range(2):
-            @pl.loop(0, 14)
-            def _(i):
-                dd_desc(p, dirn, i).wait_recv()
+    def dd_wait(p, dirn, i):
+        blk = ubuf.at[p, 0, 0]
+        rcopy(blk, blk, dd_s.at[p, dirn, i], dd_r.at[p, dirn, i], z, ok).wait_recv()
+
+    def sel_step(p):
+        def step(n):
+            d, dirn = _div(n + 1, 2), _rem(n + 1, 2)
+
+            @pl.when((n >= 1) & (n < 7))
+            def _():
+                @pl.loop(0, 4)
+                def _(j):
+                    dd_wait(p, dirn, 4 * (d - 1) + j)
+
+            @pl.when(n == 7)
+            def _():
+                for j in (12, 13):
+                    for q in range(2):
+                        dd_wait(p, q, j)
+
+            select(p, _rem(z + Z + jnp.where(dirn == 0, -d, d), Z))
+        return step
 
     def key_hits(p, zs, j, base, n):
         keys = kg[p, zs, j:j + 1, :].astype(jnp.int32)
@@ -286,22 +305,26 @@
                 rs_desc(p, dirn, i).start()
         return ev
 
-    def m_desc(p):
-        return rcopy(ms.at[p], mr, m_s.at[0], m_r.at[0], z, ok)
+    def m_desc(p, c):
+        return rcopy(ms.at[p, c], mr.at[c], m_s.at[c], m_r.at[c], z, ok)
 
     def rs_final(p):
+        @pl.loop(0, 4)
+        def _(c):
+            ms[p, c] = combine(p, z, c)
+
         @pl.loop(0, 4)
         def _(s):
             c = _rem(s + 2, 4)
             rs_desc(p, 0, 10 + s).wait_recv()
-            ms[p, c] = combine(p, z, c) + rb[p, 0, 14 + s]
-
-        @pl.loop(0, 4)
-        def _(c):
-            rs_desc(p, 1, 10 + c).wait_recv()
-            ms[p, c] = ms[p, c] + rb[p, 1, 14 + c]
-
-        pl.when(k != p)(lambda: m_desc(p).start())
+            ms[p, c] = ms[p, c] + rb[p, 0, 14 + s]
+            rs_desc(p, 1, 10 + s).wait_recv()
+            ms[p, s] = ms[p, s] + rb[p, 1, 14 + s]
+
+            @pl.when((s >= 2) & (k != p))
+            def _():
+                m_desc(p, c).start()
+                m_desc(p, s).start()
 
     def y_desc(p, c):
         return rcopy(ys.at[p, ok, c], yr.at[p, c], y_s.at[p, c], y_r.at[p, c], z, ok)
@@ -356,132 +379,160 @@
         h3 = _dot(xe, wbuf[slot, D:2 * D])
         hid[e, :, cols(j)] = (_silu(h1) * h3).astype(BF)
 
-    def e2_body(p):
+    def e2_body(p, send=True):
         def body(i, slot):
             half, c = e2_col(i)
             for e in range(EL):
                 r = _dot(hid[e], wbuf[slot, e * FE:(e + 1) * FE]).astype(BF)
                 for zs in range(Z):
                     ys[p, half, c, zs, e * CAP:(e + 1) * CAP, :] = r[zs * CAP:(zs + 1) * CAP]
-            pl.when(_rem(i, 2) == 0)(lambda: y_desc(p, c).start())
+            if send:
+                pl.when(_rem(i, 2) == 0)(lambda: y_desc(p, c).start())
         return body
+
 
     barrier = pltpu.get_barrier_semaphore()
     for zz, kk in ((right, k), (left, k), (z, ok)):
         pl.semaphore_signal(barrier, inc=1, device_id=dev(zz, kk), device_id_type=MESH)
-
+    wr_copy = pltpu.make_async_copy(wr, wrv, wr_sem.at[0])
+    wr_copy.start()
     for t in range(NS):
         issue(t, [ph_qkv])
 
     @pl.loop(0, RC)
     def _(r):
         rows = pl.ds(pl.multiple_of(r * 16, 16), 16)
-        hf = h0[rows, :].astype(F32)
-        ubuf[k, z, r] = _rms_rows(hf, nm[...].astype(F32))
-        xn[rows, :] = _rms_rows(hf, na[...].astype(F32))
-
-    lt = _dot(ubuf[k, z].reshape(T, D), wr[...]).T
+        ubuf[k, z, r] = _rms_rows(h0[rows, :].astype(F32), row(nm))
+
+    pl.semaphore_wait(barrier, 3)
+
+    @pl.when(k == 0)
+    def _():
+        own_desc(0, 0).start()
+        ag_send_own(0)
+
+    @pl.when(k == 1)
+    def _():
+        own_desc(1, 0).start()
+
+    wr_copy.wait()
+    lt = _dot(ubuf[k, z].reshape(T, D), wrv[...]).T
     rows = []
     for j in range(8):
-        hit = lax.broadcasted_iota(jnp.int32, lt.shape, 0) == idxt[j:j + 1, :]
+        hit = lax.broadcasted_iota(jnp.int32, lt.shape, 0) == idx[j:j + 1, :]
         rows.append(jnp.sum(jnp.where(hit, lt, 0.0), axis=0, keepdims=True))
     sel = jnp.concatenate(rows, axis=0)
     ex = jnp.exp(sel - jnp.max(sel, axis=0, keepdims=True))
-    kg[k, z, 0:8, :] = keyt[...].astype(F32)
+    kg[k, z, 0:8, :] = (idx[...] * CAP + slot[...]).astype(F32)
     kg[k, z, 8:16, :] = ex / jnp.sum(ex, axis=0, keepdims=True)
 
-    pl.semaphore_wait(barrier, 3)
+    @pl.when(k == 1)
+    def _():
+        own_desc(0, 0).wait_recv()
+        ag_send_own(0)
+
     for p in range(2):
-        @pl.when(k == p)
-        def _():
-            for c in own_descs(p):
-                c.start()
-    ag_begin(0)
+        pl.when(k == p)(lambda: own_desc(p, 1).start())
+
+    @pl.loop(0, RC)
+    def _(r):
+        rows = pl.ds(pl.multiple_of(r * 16, 16), 16)
+        xn[rows, :] = _rms_rows(h0[rows, :].astype(F32), row(na))
+
+    pl.when(k == 1)(lambda: own_desc(0, 1).wait_recv())
+    kg_send_own(0)
 
     ag0, ag1 = ag_event(0), ag_event(1)
     rs0, rs1 = rs_event(0), rs_event(1)
-
-    run(ph_qkv, qkv_body, lambda i: at(i, 3, 2, 3, ag0, 0))
+    sel0, sel1 = sel_step(0), sel_step(1)
+
+    run(ph_qkv, qkv_body, lambda i: at(i, 3, 2, 4, ag0, 0))
 
     @pl.loop(0, nkv)
     def _(g):
         attn(g)
-        ag0(3 + g)
-
-    run(ph_wo, wo_body, lambda i: at(i, 1, 2, 4, ag0, 7))
-    ag_begin(1)
+        at(g, 0, 2, 2, ag0, 4)
+
+    run(ph_wo, wo_body, lambda i: at(i, 0, 2, 4, ag0, 6))
+
+    @pl.when(k == 0)
+    def _():
+        for q in range(2):
+            own_desc(1, q).wait_recv()
+    ag_send_own(1)
+    kg_send_own(1)
 
     @pl.loop(0, RC)
     def _(r):
         rows = pl.ds(pl.multiple_of(r * 16, 16), 16)
-        xn[rows, :] = _rms_rows(a[rows, :].astype(F32), nf[...].astype(F32))
-
-    run(ph_13a, w13_body(0), lambda i: at(i, 1, 2, 3, ag0, 11))
-    ag_drain(0)
-
-    @pl.loop(0, Z)
-    def _(zs):
-        select(0, zs)
-
-    run(ph_e1[0], e1_body, lambda i: at(i, 0, 2, 12, ag1, 0))
-
-    @pl.loop(0, Z)
-    def _(zs):
-        gates(0, zs)
-
-    run(ph_e2[0], e2_body(0), lambda i: at(i, 0, 2, 2, ag1, 12))
-    for c in range(4):
-        y_desc(0, c).wait_recv()
-
-    @pl.loop(0, 4)
-    def _(i):
-        rs0(i)
-
-    ag_drain(1)
-
-    @pl.loop(0, Z)
-    def _(zs):
-        select(1, zs)
-        gates(1, zs)
-
-    run(ph_e1[1], e1_body, lambda i: at(i, 1, 4, 6, rs0, 4))
-    run(ph_e2[1], e2_body(1), lambda i: at(i, 2, 3, 2, rs0, 10))
-    for c in range(4):
-        y_desc(1, c).wait_recv()
-
-    @pl.loop(12, 14)
-    def _(i):
-        rs0(i)
-
-    @pl.loop(0, 4)
-    def _(i):
-        rs1(i)
+        xn[rows, :] = _rms_rows(a[rows, :].astype(F32), row(nf))
+
+    def ev_13a(i):
+        at(i, 0, 2, 3, ag0, 10)
+        at(i, 0, 1, 5, sel0, 0)
+    run(ph_13a, w13_body(0), ev_13a)
+    ag0(13)
+    pl.loop(5, 8)(sel0)
+
+    def ev_e10(i):
+        at(i, 0, 2, 12, ag1, 0)
+        at(i, 1, 2, 8, lambda n: gates(0, n), 0)
+    run(ph_e1[0], e1_body, ev_e10)
+
+    def rs_open(p, rs, half):
+        for c in (half, half + 2):
+            y_desc(p, c).wait_recv()
+        pl.loop(0, 2)(lambda n: rs(2 * n + half))
+
+    def ev_e20(i):
+        at(i, 0, 1, 2, ag1, 12)
+        pl.when(i == 4)(lambda: rs_open(0, rs0, 0))
+    run(ph_e2[0], e2_body(0), ev_e20)
+    rs_open(0, rs0, 1)
+    pl.loop(0, 8)(sel1)
+    rs0(4)
+
+    def ev_e11(i):
+        at(i, 2, 4, 6, rs0, 5)
+        at(i, 1, 2, 8, lambda n: gates(1, n), 0)
+    run(ph_e1[1], e1_body, ev_e11)
+
+    def ev_e21(i):
+        at(i, 1, 3, 2, rs0, 11)
+        pl.when(i == 6)(lambda: rs_open(1, rs1, 0))
+    run(ph_e2[1], e2_body(1), ev_e21)
+    rs0(13)
+    rs_open(1, rs1, 1)
 
     run(ph_13b, w13_body(n13a))
     rs_final(0)
-    run(ph_2, w2_body, lambda i: at(i, 0, 2, 4, rs1, 4))
-
-    @pl.loop(8, 14)
-    def _(i):
-        rs1(i)
-
+    run(ph_2, w2_body, lambda i: at(i, 0, 3, 3, rs1, 4))
+    pl.loop(7, 14)(rs1)
     rs_final(1)
-    pl.when(k == 0)(lambda: m_desc(0).wait_recv())
-    pl.when(k == 1)(lambda: m_desc(1).wait_recv())
 
     @pl.loop(0, 4)
     def _(c):
         own = cols(k * NCH + c)
         out[:, own] = (a[:, own].astype(F32) + f[:, own] + ms[k, c]).astype(BF)
+
+    @pl.loop(0, 4)
+    def _(n):
+        c = _rem(n, 2) * 2 + _div(n, 2)
+        m_desc(0, c).wait_recv()
         oth = cols(ok * NCH + c)
         out[:, oth] = (a[:, oth].astype(F32) + f[:, oth] + mr[c]).astype(BF)
 
     for p in range(2):
         @pl.when(k == p)
         def _():
-            for c in own_descs(p):
-                c.wait_send()
-        pl.when(k != p)(lambda: m_desc(p).wait_send())
+            for q in range(2):
+                own_desc(p, q).wait_send()
+
+        @pl.when(k != p)
+        def _():
+            for c in range(4):
+                m_desc(p, c).wait_send()
+
         for dirn in range(2):
             @pl.loop(0, 14)
             def _(i):
@@ -510,8 +561,6 @@
         cap = 2 * t * kt // e
         Z = G // 2
         nq, nk, ff, fe = wq.shape[1], wk.shape[1], w1.shape[1], ue1.shape[2]
-        keyt = (idx * cap + slot).reshape(t, kt).T
-        idxt = idx.reshape(t, kt).T
         pos = np.arange(s, dtype=np.float64)
         inv = ROPE_BASE ** (-2.0 * np.arange(HEAD // 2, dtype=np.float64) / HEAD)
         ang = pos[:, None] * inv[None, :]
@@ -522,44 +571,50 @@
         vm = pl.BlockSpec(memory_space=pltpu.VMEM)
         hb = pl.BlockSpec(memory_space=pl.ANY)
         V, DMA = pltpu.VMEM, pltpu.SemaphoreType.DMA
-        kern = functools.partial(_kernel, Z, t, d, nq, nk, ff, el, fe, cap)
-        out = pl.pallas_call(
-            kern,
-            out_shape=jax.ShapeDtypeStruct((t, d), BF),
-            in_specs=[vm] * 9 + [hb] * 10,
-            out_specs=vm,
-            scratch_shapes=[
-                V((2, Z, t // 16, 16, d), BF),
-                V((2, Z, 16, t), F32),
-                V((el, Z, cap, d), BF),
-                V((el, Z * cap, fe), BF),
-                V((2, 2, 4, Z, nslot, TN), BF),
-                V((2, 4, Z, nslot, TN), BF),
-                V((2, Z, 3 * t, 2 * nslot), BF),
-                V((2, 2, 18, t, TN), F32),
-                V((2, 4, t, TN), F32),
-                V((4, t, TN), F32),
-                V((NS, rows, TN), BF),
-                V((t, d), BF),
-                V((t, nq + 2 * nk), BF),
-                V((t, nq), BF),
-                V((t, d), BF),
-                V((t, ff), BF),
-                V((t, d), F32),
-                DMA((NS, 8)),
-                DMA((2,)), DMA((2,)),
-                DMA((2, 2, 14)), DMA((2, 2, 14)),
-                DMA((2, 2, 4)), DMA((2, 2, 4)),
-                DMA((2, 2, 14)), DMA((2, 2, 14)),
-                DMA((2, 4)), DMA((2, 4)),
-                DMA((2, 2, 14)), DMA((2, 2, 14)),
-                DMA((1,)), DMA((1,)),
-            ],
-            compiler_params=pltpu.CompilerParams(
-                collective_id=0, has_side_effects=True, vmem_limit_bytes=VMEM_LIMIT),
-            name="layer_pair",
-        )(h0.reshape(t, d), keyt, idxt, na.reshape(1, d), nf.reshape(1, d), nm.reshape(1, d), wr,
-          jnp.asarray(cosr), jnp.asarray(sinr), wq, wk, wv, wo, w1, w3, w2, ue1, ue3, ue2)
+        operands = (h0.reshape(t, d), idx.reshape(t, kt).T, slot.reshape(t, kt).T, na, nf, nm,
+                    jnp.asarray(cosr), jnp.asarray(sinr), wr, wq, wk, wv, wo, w1, w3, w2, ue1, ue3, ue2)
+
+        def call(cid):
+            kern = functools.partial(_kernel, Z, t, d, nq, nk, ff, el, fe, cap)
+            return pl.pallas_call(
+                kern,
+                out_shape=jax.ShapeDtypeStruct((t, d), BF),
+                in_specs=[vm] * 8 + [hb] * 11,
+                out_specs=vm,
+                scratch_shapes=[
+                    V((2, Z, t // 16, 16, d), BF),
+                    V((2, Z, 16, t), F32),
+                    V((el, Z, cap, d), BF),
+                    V((el, Z * cap, fe), BF),
+                    V((2, 2, 4, Z, nslot, TN), BF),
+                    V((2, 4, Z, nslot, TN), BF),
+                    V((2, Z, 3 * t, 2 * nslot), BF),
+                    V((2, 2, 18, t, TN), F32),
+                    V((2, 4, t, TN), F32),
+                    V((4, t, TN), F32),
+                    V((NS, rows, TN), BF),
+                    V((t, d), BF),
+                    V((t, nq + 2 * nk), BF),
+                    V((t, nq), BF),
+                    V((t, d), BF),
+                    V((t, ff), BF),
+                    V((t, d), F32),
+                    V((d, e), BF),
+                    DMA((NS, 8)), DMA((1,)),
+                    DMA((2,)), DMA((2,)),
+                    DMA((2, 2, 14)), DMA((2, 2, 14)),
+                    DMA((2, 2, 4)), DMA((2, 2, 4)),
+                    DMA((2, 2, 14)), DMA((2, 2, 14)),
+                    DMA((2, 4)), DMA((2, 4)),
+                    DMA((2, 2, 14)), DMA((2, 2, 14)),
+                    DMA((4,)), DMA((4,)),
+                ],
+                compiler_params=pltpu.CompilerParams(
+                    collective_id=cid, has_side_effects=True, vmem_limit_bytes=VMEM_LIMIT),
+                name="layer_pair",
+            )(*operands)
+
+        out = call(0)
         return out.reshape(b, s, d)
 
     rows_spec = P(('dp', 'ep'))

time: 163 us -> 155 us (0.951)
  local copies, waits for them, and re-layouts: 5.74 us -> 1.88 us
  Pallas kernels: 156 us -> 153 us
    reshape x3 -> x0, local copies, waits for them, and re-layouts: 3.86 us -> none  [the longest x1 1.29 us: local(): na.reshape(1, d)]
    pallas_call x1, Pallas kernels: 156 us -> 153 us  [call(): pl.pallas_call(kern, out_shape=jax.ShapeDtypeStruct((t, d), BF), in_specs...]
where the time goes in v2:
time: 155 us
  Pallas kernels  153 us (99%)
  local copies, waits for them, and re-layouts  1.88 us (1%)
    pallas_call x1, Pallas kernels, call(): pl.pallas_call(kern, out_shape=jax.ShapeDtypeStruct((t, d), BF), in_specs...  153 us

profile of v2, /device:TPU:21, one launch (start us, length us, event | category | flops | bytes accessed | tf_op | source)
XLA Modules:
  0.0 154.8 jit_solution(10036700127972091316)
XLA Ops:
  0.0 152.9 %layer_pair.1 = bf16[128,2048]{1,0:T(8,128)(2,1)} custom-call(bf16[128,2048]{1,0:T(8,128)(2,1)} %bitcast.9, s32[8,128]{1,0:T(8,128)} %bitcast.10, s32[8,128]{1,0:T(8,128)} %bitcast.11, bf16[2048]{0:T(1024)(128)(2,1)} %na.1, bf16[2048]{0:T(1024)(128)(2,1)} %nf.1, bf16[2048]{0:T(1024)(128)(2,1)} %nm.1, f32[128,128]{1,0:T(8,128)} %constant.4.clone.cosr, ...), custom_call_target="tpu_custom_call" | custom-call | tf_op jit(solution)/shard_map/layer_pair/pallas_call | solution.py:579
  152.9 1.9 %copy.21 = bf16[1,128,2048]{2,1,0:T(8,128)(2,1)} copy(bf16[1,128,2048]{2,1,0:T(8,128)(2,1)} %bitcast.8) | data formatting | bytes 1048576

commit v3 on v2

--- a/solution.py
+++ b/solution.py
@@ -95,11 +95,9 @@
     def wo_copies(i, slot):
         return [(None, lambda: pltpu.make_async_copy(wo.at[:, cols(i)], wslot(slot, 0, NQ), wsem.at[slot, 0]))]
 
-    def w13_copies(i0):
-        def go(i, slot):
-            return [(None, lambda: pltpu.make_async_copy(w1.at[:, cols(i + i0)], wslot(slot, 0, D), wsem.at[slot, 0])),
-                    (None, lambda: pltpu.make_async_copy(w3.at[:, cols(i + i0)], wslot(slot, D, D), wsem.at[slot, 1]))]
-        return go
+    def w13_copies(i, slot):
+        return [(None, lambda: pltpu.make_async_copy(w1.at[:, cols(i)], wslot(slot, 0, D), wsem.at[slot, 0])),
+                (None, lambda: pltpu.make_async_copy(w3.at[:, cols(i)], wslot(slot, D, D), wsem.at[slot, 1]))]
 
     def w2_copies(i, slot):
         return [(None, lambda: pltpu.make_async_copy(w2.at[:, cols(i)], wslot(slot, 0, FF), wsem.at[slot, 0]))]
@@ -123,15 +121,13 @@
             ue2.at[e, :, cols(half * NCH + c)], wslot(slot, e * FE, FE), wsem.at[slot, e])) for e in range(EL)]
 
     n13 = FF // TN
-    n13a = n13 // 4
     ph_qkv = Phase(nq2 + 2 * nk2, qkv_copies)
     ph_wo = Phase(D // TN, wo_copies)
-    ph_13a = Phase(n13a, w13_copies(0))
     ph_e1 = [Phase(EL * NJ, e1_copies), Phase(EL * NJ, e1_copies)]
     ph_e2 = [Phase(NC, e2_copies), Phase(NC, e2_copies)]
-    ph_13b = Phase(n13 - n13a, w13_copies(n13a))
+    ph_13 = Phase(n13, w13_copies)
     ph_2 = Phase(D // TN, w2_copies)
-    order = [ph_qkv, ph_wo, ph_13a, ph_e1[0], ph_e2[0], ph_e1[1], ph_e2[1], ph_13b, ph_2]
+    order = [ph_qkv, ph_wo, ph_e1[0], ph_e2[0], ph_e1[1], ph_e2[1], ph_13, ph_2]
     total = 0
     for q, ph in enumerate(order):
         ph.start, ph.pos = total, q
@@ -195,8 +191,8 @@
 
     NKG = (4, 3)
 
-    def ag_send_own(p):
-        for i in range(4):
+    def ag_send_own(p, half):
+        for i in (2 * half, 2 * half + 1):
             for dirn in range(2):
                 ag_desc(p, dirn, i).start()
 
@@ -218,6 +214,13 @@
                     kg_desc(p, dirn, q).wait_recv()
                     pl.when(q + 1 < NKG[dirn])(lambda: kg_desc(p, dirn, q + 1).start())
         return ev
+
+    def ag_pair(p):
+        ev = ag_event(p)
+
+        def pair(n):
+            pl.loop(0, 2)(lambda q: ev(2 * n + q))
+        return pair
 
     def dd_wait(p, dirn, i):
         blk = ubuf.at[p, 0, 0]
@@ -285,7 +288,9 @@
                      nbr[dirn], k)
 
     def rs_event(p):
-        def ev(i):
+        def ev(n):
+            r = _rem(n, 4)
+            i = jnp.where((r == 1) & (n < 12), n + 1, jnp.where((r == 2) & (n < 12), n - 1, n))
             j = i + 2
             d = 4 - _div(j, 4)
             for dirn in range(2):
@@ -362,12 +367,10 @@
         r = _dot(o[...], wbuf[slot, :NQ])
         a[:, cols(i)] = (h0[:, cols(i)].astype(F32) + r).astype(BF)
 
-    def w13_body(i0):
-        def body(i, slot):
-            h1 = _dot(xn[...], wbuf[slot, :D])
-            h3 = _dot(xn[...], wbuf[slot, D:2 * D])
-            fh[:, cols(i + i0)] = (_silu(h1) * h3).astype(BF)
-        return body
+    def w13_body(i, slot):
+        h1 = _dot(xn[...], wbuf[slot, :D])
+        h3 = _dot(xn[...], wbuf[slot, D:2 * D])
+        fh[:, cols(i)] = (_silu(h1) * h3).astype(BF)
 
     def w2_body(i, slot):
         f[:, cols(i)] = _dot(fh[...], wbuf[slot, :FF])
@@ -409,7 +412,7 @@
     @pl.when(k == 0)
     def _():
         own_desc(0, 0).start()
-        ag_send_own(0)
+        ag_send_own(0, 0)
 
     @pl.when(k == 1)
     def _():
@@ -426,10 +429,12 @@
     kg[k, z, 0:8, :] = (idx[...] * CAP + slot[...]).astype(F32)
     kg[k, z, 8:16, :] = ex / jnp.sum(ex, axis=0, keepdims=True)
 
+    pl.when(k == 0)(lambda: ag_send_own(0, 1))
+
     @pl.when(k == 1)
     def _():
         own_desc(0, 0).wait_recv()
-        ag_send_own(0)
+        ag_send_own(0, 0)
 
     for p in range(2):
         pl.when(k == p)(lambda: own_desc(p, 1).start())
@@ -442,53 +447,60 @@
     pl.when(k == 1)(lambda: own_desc(0, 1).wait_recv())
     kg_send_own(0)
 
-    ag0, ag1 = ag_event(0), ag_event(1)
+    ag0, ag1 = ag_pair(0), ag_pair(1)
     rs0, rs1 = rs_event(0), rs_event(1)
     sel0, sel1 = sel_step(0), sel_step(1)
 
-    run(ph_qkv, qkv_body, lambda i: at(i, 3, 2, 4, ag0, 0))
+    def ev_qkv(i):
+        pl.when((i == 1) & (k == 1))(lambda: ag_send_own(0, 1))
+        at(i, 3, 4, 2, ag0, 0)
+    run(ph_qkv, qkv_body, ev_qkv)
 
     @pl.loop(0, nkv)
     def _(g):
         attn(g)
-        at(g, 0, 2, 2, ag0, 4)
-
-    run(ph_wo, wo_body, lambda i: at(i, 0, 2, 4, ag0, 6))
+        at(g, 1, 2, 1, ag0, 2)
+
+    def ev_wo(i):
+        at(i, 1, 4, 2, ag0, 3)
+        at(i, 2, 1, 3, sel0, 0)
+    run(ph_wo, wo_body, ev_wo)
 
     @pl.when(k == 0)
     def _():
         for q in range(2):
             own_desc(1, q).wait_recv()
-    ag_send_own(1)
-    kg_send_own(1)
+    pl.loop(3, 5)(sel0)
 
     @pl.loop(0, RC)
     def _(r):
         rows = pl.ds(pl.multiple_of(r * 16, 16), 16)
         xn[rows, :] = _rms_rows(a[rows, :].astype(F32), row(nf))
 
-    def ev_13a(i):
-        at(i, 0, 2, 3, ag0, 10)
-        at(i, 0, 1, 5, sel0, 0)
-    run(ph_13a, w13_body(0), ev_13a)
-    ag0(13)
-    pl.loop(5, 8)(sel0)
+    ag0(5)
+    pl.loop(5, 7)(sel0)
+    ag0(6)
+    ag_send_own(1, 0)
+    kg_send_own(1)
+    sel0(7)
 
     def ev_e10(i):
-        at(i, 0, 2, 12, ag1, 0)
+        pl.when(i == 1)(lambda: ag_send_own(1, 1))
+        at(i, 4, 4, 5, ag1, 0)
         at(i, 1, 2, 8, lambda n: gates(0, n), 0)
     run(ph_e1[0], e1_body, ev_e10)
 
     def rs_open(p, rs, half):
         for c in (half, half + 2):
             y_desc(p, c).wait_recv()
-        pl.loop(0, 2)(lambda n: rs(2 * n + half))
+        pl.loop(2 * half, 2 * half + 2)(rs)
 
     def ev_e20(i):
-        at(i, 0, 1, 2, ag1, 12)
+        pl.when(i == 0)(lambda: ag1(5))
         pl.when(i == 4)(lambda: rs_open(0, rs0, 0))
     run(ph_e2[0], e2_body(0), ev_e20)
     rs_open(0, rs0, 1)
+    ag1(6)
     pl.loop(0, 8)(sel1)
     rs0(4)
 
@@ -504,10 +516,10 @@
     rs0(13)
     rs_open(1, rs1, 1)
 
-    run(ph_13b, w13_body(n13a))
+    run(ph_13, w13_body, lambda i: at(i, 18, 4, 2, rs1, 4))
     rs_final(0)
-    run(ph_2, w2_body, lambda i: at(i, 0, 3, 3, rs1, 4))
-    pl.loop(7, 14)(rs1)
+    run(ph_2, w2_body, lambda i: at(i, 0, 3, 3, rs1, 6))
+    pl.loop(9, 14)(rs1)
     rs_final(1)
 
     @pl.loop(0, 4)

time: 155 us -> 155 us (level)
  no operation moved by 1% of the time
where the time goes in v3:
time: 155 us
  Pallas kernels  153 us (99%)
  local copies, waits for them, and re-layouts  1.88 us (1%)
    pallas_call x1, Pallas kernels, call(): pl.pallas_call(kern, out_shape=jax.ShapeDtypeStruct((t, d), BF), in_specs...  153 us

profile of v3, /device:TPU:21, one launch (start us, length us, event | category | flops | bytes accessed | tf_op | source)
XLA Modules:
  0.0 155.3 jit_solution(2606426188749795254)
XLA Ops:
  0.0 153.4 %layer_pair.1 = bf16[128,2048]{1,0:T(8,128)(2,1)} custom-call(bf16[128,2048]{1,0:T(8,128)(2,1)} %bitcast.9, s32[8,128]{1,0:T(8,128)} %bitcast.10, s32[8,128]{1,0:T(8,128)} %bitcast.11, bf16[2048]{0:T(1024)(128)(2,1)} %na.1, bf16[2048]{0:T(1024)(128)(2,1)} %nf.1, bf16[2048]{0:T(1024)(128)(2,1)} %nm.1, f32[128,128]{1,0:T(8,128)} %constant.4.clone.cosr, ...), custom_call_target="tpu_custom_call" | custom-call | tf_op jit(solution)/shard_map/layer_pair/pallas_call | solution.py:591
  153.4 1.9 %copy.21 = bf16[1,128,2048]{2,1,0:T(8,128)(2,1)} copy(bf16[1,128,2048]{2,1,0:T(8,128)(2,1)} %bitcast.8) | data formatting | bytes 1048576
